TPU v7x, 32 devices: a whole 2x2x4 slice. The times are simulated.
32 devices in a mesh: pipe: 4 (over z), expert: 4 (over y, x), tensor: 2 (over core).
Axes of the slice: x: 2, y: 2, z: 4, core: 2. Of those that a mesh axis runs over, the one named last changes fastest.
Arguments:
- inputs_prev: bfloat16 [4, 512, 3584], P('pipe', 'expert', 'tensor'), may hold values from -6 to 6
- cotangent_next: bfloat16 [4, 512, 3584], P('pipe', 'expert', 'tensor'), may hold values from -6 to 6
- saved_input: bfloat16 [4, 512, 3584], P('pipe', 'expert', 'tensor'), may hold values from -6 to 6
- expert_ids: int32 [2, 4, 512, 8], P(None, 'pipe', 'expert'), may hold values from 0 to 255, as said below
- keep_mask: int32 [2, 4, 512, 8], P(None, 'pipe', 'expert'), may hold values from 0 to 1, as said below
- slot_pos: int32 [2, 4, 512, 8], P(None, 'pipe', 'expert'), may hold values from 0 to 3, as said below
- weight_q: int32 [2, 4, 512, 8], P(None, 'pipe', 'expert'), may hold values from 1 to 4095
- gate_routed: bfloat16 [4, 4, 3584, 512], P('pipe', 'expert', None, 'tensor'), may hold values from -0.09375 to 0.09375
- up_routed: bfloat16 [4, 4, 3584, 512], P('pipe', 'expert', None, 'tensor'), may hold values from -0.09375 to 0.09375
- down_routed: bfloat16 [4, 4, 512, 3584], P('pipe', 'expert', 'tensor'), may hold values from -0.1875 to 0.1875
- gate_shared: bfloat16 [4, 3584, 1024], P('pipe', None, 'tensor'), may hold values from -0.09375 to 0.09375
- up_shared: bfloat16 [4, 3584, 1024], P('pipe', None, 'tensor'), may hold values from -0.09375 to 0.09375
- down_shared: bfloat16 [4, 1024, 3584], P('pipe', 'tensor'), may hold values from -0.1875 to 0.1875
Outputs:
- out_act: bfloat16 [4, 512, 3584], P('pipe', 'expert', 'tensor')
- in_grad: bfloat16 [4, 512, 3584], P('pipe', 'expert', 'tensor')
Inputs may be any that keep to these rules, and one draw needn't show every extreme that they name: `expert_ids`: each row names 8 different experts; in every section and micro-batch one expert below 2 is named by every row. `keep_mask`: 1 only where the expert named is below 2; in one block of 128 rows no expert has more than 4 kept choices, and in every section and micro-batch one expert has exactly 4 in every block. `slot_pos`: kept choices of one block naming the same expert hold different slots; 0 where keep_mask is 0.
All inputs are finite; a program needn't handle non-finite values.
Results may differ from a plain program's by a relative error of at most 0.005.
Values may be sent and summed in bfloat16 or wider, within the bound.
A program may use at most 64 MiB of HBM per device.

v0:
```python
import jax
import jax.numpy as jnp
from jax import lax
from jax.sharding import PartitionSpec as P


def passed_along(block, axis, distance):
    devices = range(lax.axis_size(axis))
    route = [((i - distance) % len(devices), i) for i in devices]
    return lax.ppermute(block, axis, route)


def swish(values):
    return values * jax.nn.sigmoid(values)


def swish_slope(values):
    logistic = jax.nn.sigmoid(values)
    return logistic * (1.0 + values * (1.0 - logistic))


def contract_last(left, right):
    return lax.dot_general(
        left, right, (((1,), (1,)), ((), ())), preferred_element_type=jnp.float32
    )


def slot_plan(choice_ids, kept_flags, slot_index, weight_levels, total_slots, capacity):
    target = jnp.where(kept_flags > 0, choice_ids * capacity + slot_index, -1)
    slots = jnp.arange(total_slots, dtype=jnp.int32)
    match = target[None] == slots[:, None, None]
    chosen = jnp.sum(match.astype(jnp.int32), axis=2)
    level = jnp.sum(jnp.where(match, weight_levels[None], 0), axis=2)
    return (chosen.astype(jnp.bfloat16), level)


def section_link(values, offset):
    return passed_along(values, "pipe", offset)


def select_rows(chosen, values):
    return jnp.dot(chosen, values, preferred_element_type=jnp.float32)


def split_level(level):
    high = (level // 64).astype(jnp.float32) / 64.0
    low = (level % 64).astype(jnp.float32) / 4096.0
    return (high.astype(jnp.bfloat16), low.astype(jnp.bfloat16))


def combine(factors, rows):
    return lax.dot_general(
        factors, rows, (((0,), (0,)), ((), ())), preferred_element_type=jnp.float32
    )


def other_sums(total, n_tensor):
    width = total.shape[1] // n_tensor
    me = lax.axis_index("tensor")
    mine = lax.dynamic_slice_in_dim(total, me * width, width, axis=1)
    for step in range(1, n_tensor):
        to = (me + step) % n_tensor
        piece = lax.dynamic_slice_in_dim(total, to * width, width, axis=1)
        mine = mine + passed_along(piece, "tensor", step)
    return mine


def expert_local(rows_in, rows_saved, rows_cot, gate_w, up_w, down_w):
    gate_pre = jnp.dot(rows_in, gate_w, preferred_element_type=jnp.float32)
    up_pre = jnp.dot(rows_in, up_w, preferred_element_type=jnp.float32)
    hidden = (swish(gate_pre) * up_pre).astype(jnp.bfloat16)
    result = jnp.dot(hidden, down_w, preferred_element_type=jnp.float32).astype(jnp.bfloat16)
    gate_back = jnp.dot(rows_saved, gate_w, preferred_element_type=jnp.float32)
    up_back = jnp.dot(rows_saved, up_w, preferred_element_type=jnp.float32)
    grad_hidden = contract_last(rows_cot, down_w)
    grad_gate = (grad_hidden * up_back * swish_slope(gate_back)).astype(jnp.bfloat16)
    grad_up = (grad_hidden * swish(gate_back)).astype(jnp.bfloat16)
    grad_rows = (contract_last(grad_gate, gate_w) + contract_last(grad_up, up_w)).astype(
        jnp.bfloat16
    )
    return (result, grad_rows)


def shared_pass(full_in, full_saved, full_cot, gate_w, up_w, down_w):
    gate_pre = jnp.dot(full_in, gate_w, preferred_element_type=jnp.float32)
    up_pre = jnp.dot(full_in, up_w, preferred_element_type=jnp.float32)
    hidden = (swish(gate_pre) * up_pre).astype(jnp.bfloat16)
    shared_out = jnp.dot(hidden, down_w, preferred_element_type=jnp.float32)
    gate_back = jnp.dot(full_saved, gate_w, preferred_element_type=jnp.float32)
    up_back = jnp.dot(full_saved, up_w, preferred_element_type=jnp.float32)
    grad_hidden = contract_last(full_cot, down_w)
    grad_gate = (grad_hidden * up_back * swish_slope(gate_back)).astype(jnp.bfloat16)
    grad_up = (grad_hidden * swish(gate_back)).astype(jnp.bfloat16)
    shared_grad = contract_last(grad_gate, gate_w) + contract_last(grad_up, up_w)
    return (shared_out, shared_grad)


def local(
    inputs_prev,
    cotangent_next,
    saved_input,
    expert_ids,
    keep_mask,
    slot_pos,
    weight_q,
    gate_routed,
    up_routed,
    down_routed,
    gate_shared,
    up_shared,
    down_shared,
):
    capacity = inputs_prev.shape[1] // 32
    n_expert = lax.axis_size("expert")
    n_tensor = lax.axis_size("tensor")
    experts_here = n_expert // 2
    slots = experts_here * capacity
    forward_in = section_link(inputs_prev[0], 1)
    backward_in = section_link(cotangent_next[0], -1)
    chosen_f, level_f = slot_plan(
        expert_ids[0, 0], keep_mask[0, 0], slot_pos[0, 0], weight_q[0, 0], slots, capacity
    )
    chosen_b, level_b = slot_plan(
        expert_ids[1, 0], keep_mask[1, 0], slot_pos[1, 0], weight_q[1, 0], slots, capacity
    )
    gate_w = gate_routed[0, 0]
    up_w = up_routed[0, 0]
    down_w = down_routed[0, 0]
    full_saved = lax.all_gather(saved_input[0], "tensor", axis=1, tiled=True)
    full_in = lax.all_gather(forward_in, "tensor", axis=1, tiled=True)
    full_cot = lax.all_gather(backward_in, "tensor", axis=1, tiled=True)
    feature_count = full_in.shape[1]
    weight_b = jnp.sum(level_b, axis=1).astype(jnp.float32) / 4096.0
    parcel = jnp.stack(
        (
            select_rows(chosen_f, full_in).astype(jnp.bfloat16),
            select_rows(chosen_b, full_saved).astype(jnp.bfloat16),
            (weight_b[:, None] * select_rows(chosen_b, full_cot)).astype(jnp.bfloat16),
        )
    ).reshape(3, experts_here, 1, capacity, feature_count)
    parcel = jnp.broadcast_to(parcel, (3, experts_here, 2, capacity, feature_count))
    parcel = parcel.reshape(3, n_expert, capacity, feature_count)
    pieces = lax.all_to_all(parcel, "expert", split_axis=1, concat_axis=1, tiled=True)
    rows = pieces.reshape(3, n_expert * capacity, feature_count)
    result, grad_rows = expert_local(rows[0], rows[1], rows[2], gate_w, up_w, down_w)
    returned = lax.all_to_all(
        jnp.stack((result, grad_rows)).reshape(2, n_expert, capacity, feature_count),
        "expert",
        split_axis=1,
        concat_axis=1,
        tiled=True,
    )
    back = returned.reshape(2, n_expert * capacity, feature_count)

    def doubled(factors):
        spread = factors.reshape(experts_here, 1, capacity, -1)
        spread = jnp.broadcast_to(spread, (experts_here, 2) + spread.shape[2:])
        return spread.reshape(n_expert * capacity, -1)

    high_f, low_f = split_level(level_f)
    factors_f = jnp.concatenate((doubled(high_f), doubled(low_f)), axis=0)
    routed_out = combine(factors_f, jnp.concatenate((back[0], back[0]), axis=0))
    routed_grad = combine(doubled(chosen_b), back[1])
    shared_out, shared_grad = shared_pass(
        full_in, full_saved, full_cot, gate_shared[0], up_shared[0], down_shared[0]
    )
    summed_out = other_sums(routed_out + shared_out, n_tensor)
    summed_grad = other_sums(routed_grad + shared_grad, n_tensor)
    return (summed_out.astype(jnp.bfloat16)[None], summed_grad.astype(jnp.bfloat16)[None])


def solution(mesh):
    return jax.shard_map(
        local,
        mesh=mesh,
        in_specs=(
            P("pipe", "expert", "tensor"),
            P("pipe", "expert", "tensor"),
            P("pipe", "expert", "tensor"),
            P(None, "pipe", "expert", None),
            P(None, "pipe", "expert", None),
            P(None, "pipe", "expert", None),
            P(None, "pipe", "expert", None),
            P("pipe", "expert", None, "tensor"),
            P("pipe", "expert", None, "tensor"),
            P("pipe", "expert", "tensor", None),
            P("pipe", None, "tensor"),
            P("pipe", None, "tensor"),
            P("pipe", "tensor", None),
        ),
        out_specs=(P("pipe", "expert", "tensor"), P("pipe", "expert", "tensor")),
        check_vma=False,
    )
```

profile of v0, /device:TPU:0, one launch (start us, length us, event | category | flops | bytes accessed | tf_op | source)
XLA Modules:
  0.0 99.7 jit_solution(14145739943017148776)
XLA Ops:
  0.6 0.0 copy-start
  0.6 5.1 %collective-permute-start.1 = (bf16[128,1792]{1,0:T(8,128)(2,1)}, bf16[128,1792]{1,0:T(8,128)(2,1)}, u32[]{:S(2)}, u32[]{:S(2)}) collective-permute-start(bf16[128,1792]{1,0:T(8,128)(2,1)} %bitcast.127), channel_id=1, source_target_pairs={{8,0},{16,8},{24,16},{0,24},{9,1},{17,9},{25,17},{1,25},{10,2},{18... | collective-permute-start | bytes 1376264 | tf_op jit(solution)/shard_map/ppermute | solution.py:10
  5.8 0.8 slice_bitcast_fusion.1
  6.6 0.2 select_reduce_fusion
  6.8 2.7 %all-gather = bf16[1,128,3584]{2,1,0:T(8,128)(2,1)S(1)} all-gather(bf16[1,128,1792]{2,1,0:T(8,128)(2,1)} %param.15), channel_id=2, replica_groups=mesh['pipe'=4,'expert'=4,'tensor'=2] {'tensor'}, dimensions={2}, use_global_device_ids=true | all-gather | bytes 1376256 | tf_op jit(solution)/shard_map/all_gather | solution.py:129
  9.6 0.2 convolution_convert_fusion.1
  9.8 2.7 %fusion.13 = f32[128,512]{1,0:T(8,128)S(1)} fusion(bf16[1,3584,512]{2,1,0:T(8,128)(2,1)} %param.23, bf16[1,128,3584]{2,1,0:T(8,128)(2,1)S(1)} %all-gather), kind=kOutput, calls=%fused_computation.20 | convolution fusion | flops 469762048 | bytes 4849664 | tf_op jit(solution)/shard_map/dot_general | solution.py:89
  12.5 4.5 %collective-permute-done.1 = bf16[128,1792]{1,0:T(8,128)(2,1)} collective-permute-done((bf16[128,1792]{1,0:T(8,128)(2,1)}, bf16[128,1792]{1,0:T(8,128)(2,1)}, u32[]{:S(2)}, u32[]{:S(2)}) %collective-permute-start.1) | collective-permute-done | bytes 458784 | tf_op jit(solution)/shard_map/ppermute | solution.py:10
  17.0 2.7 %all_gather.11 = bf16[128,3584]{1,0:T(8,128)(2,1)S(1)} all-gather(bf16[128,1792]{1,0:T(8,128)(2,1)} %collective-permute-done.1), channel_id=1, replica_groups=mesh['pipe'=4,'expert'=4,'tensor'=2] {'tensor'}, dimensions={1}, use_global_device_ids=true | all-gather | bytes 1376256 | tf_op jit(solution)/shard_map/all_gather | solution.py:131
  19.7 0.9 fusion.2
  20.6 1.5 %stack.23 = bf16[1,2,1,4,3584]{4,3,1,2,0:T(4,128)(2,1)} reshape(bf16[8,3584]{1,0:T(8,128)(2,1)} %fusion.2) | data formatting | bytes 114688 | tf_op jit(solution)/shard_map/stack | solution.py:134
  22.1 4.4 %collective-permute-done = bf16[128,1792]{1,0:T(8,128)(2,1)S(1)} collective-permute-done((bf16[128,1792]{1,0:T(8,128)(2,1)}, bf16[128,1792]{1,0:T(8,128)(2,1)S(1)}, u32[]{:S(2)}, u32[]{:S(2)}) %collective-permute-start) | collective-permute-done | bytes 458784 | tf_op jit(solution)/shard_map/ppermute | solution.py:10
  26.5 2.5 %all_gather.9 = bf16[128,3584]{1,0:T(8,128)(2,1)S(1)} all-gather(bf16[128,1792]{1,0:T(8,128)(2,1)S(1)} %collective-permute-done), channel_id=1, replica_groups=mesh['pipe'=4,'expert'=4,'tensor'=2] {'tensor'}, dimensions={1}, use_global_device_ids=true | all-gather | bytes 1376256 | tf_op jit(solution)/shard_map/all_gather | solution.py:130
  29.0 0.2 convolution_convert_fusion.2
  29.2 1.0 maximum_bitcast_fusion
  30.2 0.1 copy.26
  30.2 0.8 broadcast_in_dim.69
  31.1 4.1 %all-to-all-start = ((bf16[3,4,4,3584]{3,2,0,1:T(4,128)(2,1)}), bf16[3,4,4,3584]{3,2,0,1:T(4,128)(2,1)}, u32[]{:S(2)}, u32[]{:S(2)}) async-start(bf16[3,4,4,3584]{3,2,0,1:T(4,128)(2,1)} %bitcast.11), calls=%async_computation | async-start | bytes 688128 | tf_op jit(solution)/shard_map/all_to_all | solution.py:143
  35.2 3.6 %fusion.3 = f32[128,512]{1,0:T(8,128)S(1)} fusion(bf16[128,3584]{1,0:T(8,128)(2,1)} %copy-done.3, bf16[1,512,3584]{2,1,0:T(8,128)(2,1)} %param.25), kind=kOutput, calls=%fused_computation.10 | convolution fusion | flops 469762048 | bytes 4849664 | tf_op jit(solution)/shard_map/dot_general | solution.py:23
  38.8 6.6 %fusion.11 = f32[128,3584]{1,0:T(8,128)} fusion(bf16[1,3584,512]{2,1,0:T(8,128)(2,1)} %param.23, f32[128,512]{1,0:T(8,128)S(1)} %fusion.3, bf16[1,3584,512]{2,1,0:T(8,128)(2,1)} %param.24, bf16[1,128,3584]{2,1,0:T(8,128)(2,1)} %copy-done.2, f32[128,512]{1,0:T(8,128)S(1)} %fusion.13), kind=kOutput, calls=%fused_computation.18 | convolution fusion | flops 940179456 | bytes 10616832 | tf_op jit(solution)/shard_map/dot_general | solution.py:23
  45.4 1.8 %fusion.112 = (bf16[1,4,4,3584]{3,2,0,1:T(4,128)(2,1)}, bf16[1,4,4,3584]{3,2,0,1:T(4,128)(2,1)S(1)}, bf16[1,4,4,3584]{3,2,0,1:T(4,128)(2,1)S(1)}) fusion(bf16[3,4,4,3584]{3,2,0,1:T(4,128)(2,1)} %all-to-all-done), kind=kLoop, calls=%fused_computation.123 | loop fusion | bytes 688128 | tf_op jit(solution)/shard_map/slice | solution.py:145
  47.1 0.7 squeeze.56
  47.9 2.2 %fusion.17 = f32[16,256]{1,0:T(8,128)S(1)} fusion(bf16[16,3584]{1,0:T(8,128)(2,1)} %squeeze.56, bf16[1,1,256,3584]{3,2,1,0:T(8,128)(2,1)} %param.22), kind=kOutput, calls=%fused_computation.24 | convolution fusion | flops 29360128 | bytes 1966080 | tf_op jit(solution)/shard_map/dot_general | solution.py:23
  50.1 0.4 fusion.27
  50.5 3.5 %fusion.25 = f32[16,3584]{1,0:T(8,128)} fusion(bf16[1,1,3584,256]{3,2,1,0:T(8,128)(2,1)} %param.20, f32[16,256]{1,0:T(8,128)S(1)} %fusion.17, bf16[16,3584]{1,0:T(8,128)(2,1)S(1)} %squeeze.57, bf16[1,1,3584,256]{3,2,1,0:T(8,128)(2,1)S(1)} %copy-done, f32[16,256]{1,0:T(8,128)S(1)} %fusion.27), kind=kOutput, calls=%fused_computation.32 | convolution fusion | flops 58761216 | bytes 4046848 | tf_op jit(solution)/shard_map/dot_general | solution.py:23
  54.0 1.5 %fusion.1 = bf16[16,3584]{1,0:T(8,128)(2,1)S(1)} fusion(f32[16,3584]{1,0:T(8,128)} %fusion.25, bf16[1,1,3584,256]{3,2,1,0:T(8,128)(2,1)S(1)} %copy-done, f32[16,256]{1,0:T(8,128)S(1)} %fusion.17, f32[16,256]{1,0:T(8,128)S(1)} %fusion.27), kind=kOutput, calls=%fused_computation.4 | convolution fusion | flops 29499392 | bytes 2211840 | tf_op jit(solution)/shard_map/dot_general | solution.py:23
  55.5 0.9 squeeze.52
  56.5 1.8 %fusion.29 = f32[16,256]{1,0:T(8,128)S(1)} fusion(bf16[16,3584]{1,0:T(8,128)(2,1)S(1)} %squeeze.52, bf16[1,1,3584,256]{3,2,1,0:T(8,128)(2,1)} %param.20), kind=kOutput, calls=%fused_computation.36 | convolution fusion | flops 29360128 | bytes 1966080 | tf_op jit(solution)/shard_map/dot_general | solution.py:69
  58.3 3.3 %convolution_convert_fusion = bf16[16,3584]{1,0:T(8,128)(2,1)} fusion(bf16[1,1,256,3584]{3,2,1,0:T(8,128)(2,1)} %param.22, bf16[16,3584]{1,0:T(8,128)(2,1)S(1)} %squeeze.52, bf16[1,1,3584,256]{3,2,1,0:T(8,128)(2,1)S(1)} %copy-done, f32[16,256]{1,0:T(8,128)S(1)} %fusion.29), kind=kOutput, calls=%fused_computation.5 | convolution fusion | flops 58802176 | bytes 3915776 | tf_op jit(solution)/shard_map/dot_general | solution.py:72
  61.6 0.9 stack.25
  62.5 0.8 pad_maximum_fusion
  63.4 4.1 %all-to-all-start.1 = ((bf16[2,4,4,3584]{3,2,0,1:T(4,128)(2,1)}), bf16[2,4,4,3584]{3,2,0,1:T(4,128)(2,1)}, u32[]{:S(2)}, u32[]{:S(2)}) async-start(bf16[2,4,4,3584]{3,2,0,1:T(4,128)(2,1)} %pad_maximum_fusion), calls=%async_computation.1 | async-start | bytes 458752 | tf_op jit(solution)/shard_map/all_to_all | solution.py:146
  67.5 2.7 %fusion.9 = f32[128,512]{1,0:T(8,128)S(1)} fusion(bf16[128,3584]{1,0:T(8,128)(2,1)S(1)} %all_gather.9, bf16[1,3584,512]{2,1,0:T(8,128)(2,1)} %param.24), kind=kOutput, calls=%fused_computation.16 | convolution fusion | flops 469762048 | bytes 4849664 | tf_op jit(solution)/shard_map/dot_general | solution.py:86
  70.2 3.0 %all-to-all-done.1 = bf16[2,4,4,3584]{3,2,0,1:T(4,128)(2,1)} async-done(((bf16[2,4,4,3584]{3,2,0,1:T(4,128)(2,1)}), bf16[2,4,4,3584]{3,2,0,1:T(4,128)(2,1)}, u32[]{:S(2)}, u32[]{:S(2)}) %all-to-all-start.1) | async-done | bytes 229408 | tf_op jit(solution)/shard_map/all_to_all | solution.py:146
  73.2 1.7 %fusion.113 = (bf16[1,4,4,3584]{3,2,0,1:T(4,128)(2,1)}, bf16[1,4,4,3584]{3,2,0,1:T(4,128)(2,1)}) fusion(bf16[2,4,4,3584]{3,2,0,1:T(4,128)(2,1)} %all-to-all-done.1), kind=kLoop, calls=%fused_computation.124 | loop fusion | bytes 458752 | tf_op jit(solution)/shard_map/slice | solution.py:163
  74.9 1.6 %squeeze.58 = bf16[16,3584]{1,0:T(8,128)(2,1)} reshape(bf16[1,4,4,3584]{3,2,0,1:T(4,128)(2,1)} %get-tuple-element.10) | data formatting | bytes 229376 | tf_op jit(solution)/shard_map/squeeze | solution.py:162
  76.5 2.6 %fusion.71 = f32[128,3584]{1,0:T(8,128)} fusion(bf16[16,3584]{1,0:T(8,128)(2,1)} %squeeze.58, bf16[16,128]{1,0:T(8,128)(2,1)S(1)} %bitcast.123, bf16[16,128]{1,0:T(8,128)(2,1)S(1)} %bitcast.124), kind=kOutput, calls=%fused_computation.61 | convolution fusion | flops 29835264 | bytes 1957888 | tf_op jit(solution)/shard_map/dot_general | solution.py:52
  79.1 6.2 %convolution_add_fusion.1 = f32[128,3584]{1,0:T(8,128)} fusion(f32[128,3584]{1,0:T(8,128)} %fusion.71, bf16[1,512,3584]{2,1,0:T(8,128)(2,1)} %param.25, f32[128,512]{1,0:T(8,128)S(1)} %fusion.9, bf16[128,3584]{1,0:T(8,128)(2,1)S(1)} %all_gather.9, bf16[1,3584,512]{2,1,0:T(8,128)(2,1)} %param.23), kind=kOutput, calls=%fused_computation.2 | convolution fusion | flops 940376064 | bytes 12189696 | tf_op jit(solution)/shard_map/dot_general | solution.py:88
  85.3 2.2 %constant_dynamic-slice_fusion = f32[128,1792]{1,0:T(8,128)} fusion(f32[128,3584]{1,0:T(8,128)} %convolution_add_fusion.1, s32[]{:T(128)S(6)} %select_n.74), kind=kLoop, calls=%fused_computation.113 | loop fusion | bytes 1835012 | tf_op jit(solution)/shard_map/dynamic_slice | solution.py:63
  87.6 0.4 fusion.114
  88.0 1.1 %copy-done.6 = f32[128,3584]{1,0:T(8,128)S(1)} copy-done((f32[128,3584]{1,0:T(8,128)S(1)}, f32[128,3584]{1,0:T(8,128)}, u32[]{:S(2)}) %copy-start.6) | copy-done | bytes 1835032
  89.1 3.4 %fusion = f32[128,3584]{1,0:T(8,128)S(1)} fusion(f32[128,3584]{1,0:T(8,128)S(1)} %fusion.114, f32[128,3584]{1,0:T(8,128)S(1)} %copy-done.6, bf16[1,3584,512]{2,1,0:T(8,128)(2,1)} %param.24, f32[128,512]{1,0:T(8,128)S(1)} %fusion.3, f32[128,512]{1,0:T(8,128)S(1)} %fusion.13), kind=kOutput, calls=%fused_computation.1 | convolution fusion | flops 471072768 | bytes 9699328 | tf_op jit(solution)/shard_map/dot_general | solution.py:23
  92.5 1.3 %copy-done.4 = f32[128,3584]{1,0:T(8,128)} copy-done((f32[128,3584]{1,0:T(8,128)}, f32[128,3584]{1,0:T(8,128)S(1)}, u32[]{:S(2)}) %copy-start.4) | copy-done | bytes 1835032
  93.7 1.0 %constant_dynamic-slice_fusion.1 = f32[128,1792]{1,0:T(8,128)} fusion(f32[128,3584]{1,0:T(8,128)S(1)} %fusion, s32[]{:T(128)S(6)} %select_n.74), kind=kLoop, calls=%fused_computation.114 | loop fusion | bytes 1835012 | tf_op jit(solution)/shard_map/dynamic_slice | solution.py:63
  94.7 0.5 collective-permute-start.3
  95.2 2.2 %fusion.65 = bf16[1,128,1792]{2,1,0:T(8,128)(2,1)} fusion(f32[128,1792]{1,0:T(8,128)S(1)} %collective-permute-done.2, f32[128,3584]{1,0:T(8,128)} %convolution_add_fusion.1, s32[]{:T(128)S(6)} %select_n.72), kind=kLoop, calls=%fused_computation.51 | loop fusion | flops 458752 | bytes 2293764 | tf_op jit(solution)/shard_map/broadcast_in_dim | solution.py:169
  97.4 0.3 collective-permute-done.3
  97.7 2.0 %fusion.66 = bf16[1,128,1792]{2,1,0:T(8,128)(2,1)} fusion(f32[128,1792]{1,0:T(8,128)} %collective-permute-done.3, f32[128,3584]{1,0:T(8,128)S(1)} %copy-done.5, s32[]{:T(128)S(6)} %select_n.72), kind=kLoop, calls=%fused_computation.52 | loop fusion | flops 458752 | bytes 2293764 | tf_op jit(solution)/shard_map/broadcast_in_dim | solution.py:169
  (29 shorter events, 0.3 us)
Async XLA Ops:
  0.6 49.9 %copy-start = (bf16[1,1,3584,256]{3,2,1,0:T(8,128)(2,1)S(1)}, bf16[1,1,3584,256]{3,2,1,0:T(8,128)(2,1)}, u32[]{:S(2)}) copy-start(bf16[1,1,3584,256]{3,2,1,0:T(8,128)(2,1)} %param.21) | copy-start | bytes 5505028
  0.6 16.4 %collective-permute-start.1 = (bf16[128,1792]{1,0:T(8,128)(2,1)}, bf16[128,1792]{1,0:T(8,128)(2,1)}, u32[]{:S(2)}, u32[]{:S(2)}) collective-permute-start(bf16[128,1792]{1,0:T(8,128)(2,1)} %bitcast.127), channel_id=1, source_target_pairs={{8,0},{16,8},{24,16},{0,24},{9,1},{17,9},{25,17},{1,25},{10,2},{18... | collective-permute-start | bytes 1376264 | tf_op jit(solution)/shard_map/ppermute | solution.py:10
  5.8 20.7 %collective-permute-start = (bf16[128,1792]{1,0:T(8,128)(2,1)}, bf16[128,1792]{1,0:T(8,128)(2,1)S(1)}, u32[]{:S(2)}, u32[]{:S(2)}) collective-permute-start(bf16[128,1792]{1,0:T(8,128)(2,1)} %bitcast.128), channel_id=1, source_target_pairs={{24,0},{0,8},{8,16},{16,24},{25,1},{1,9},{9,17},{17,25},{26,2},{2,... | collective-permute-start | bytes 1376264 | tf_op jit(solution)/shard_map/ppermute | solution.py:10
  9.5 3.0 %copy-start.2 = (bf16[1,128,3584]{2,1,0:T(8,128)(2,1)}, bf16[1,128,3584]{2,1,0:T(8,128)(2,1)S(1)}, u32[]{:S(2)}) copy-start(bf16[1,128,3584]{2,1,0:T(8,128)(2,1)S(1)} %all-gather) | copy-start | bytes 2752516
  19.7 2.4 %copy-start.3 = (bf16[128,3584]{1,0:T(8,128)(2,1)}, bf16[128,3584]{1,0:T(8,128)(2,1)S(1)}, u32[]{:S(2)}) copy-start(bf16[128,3584]{1,0:T(8,128)(2,1)S(1)} %all_gather.11) | copy-start | bytes 2752516
  31.1 14.3 %all-to-all-start = ((bf16[3,4,4,3584]{3,2,0,1:T(4,128)(2,1)}), bf16[3,4,4,3584]{3,2,0,1:T(4,128)(2,1)}, u32[]{:S(2)}, u32[]{:S(2)}) async-start(bf16[3,4,4,3584]{3,2,0,1:T(4,128)(2,1)} %bitcast.11), calls=%async_computation | async-start | bytes 688128 | tf_op jit(solution)/shard_map/all_to_all | solution.py:143
  47.8 2.3 %copy-start.1 = (bf16[1,1,3584,256]{3,2,1,0:T(8,128)(2,1)S(1)}, bf16[1,1,3584,256]{3,2,1,0:T(8,128)(2,1)}, u32[]{:S(2)}) copy-start(bf16[1,1,3584,256]{3,2,1,0:T(8,128)(2,1)} %param.20) | copy-start | bytes 5505028
  63.4 9.8 %all-to-all-start.1 = ((bf16[2,4,4,3584]{3,2,0,1:T(4,128)(2,1)}), bf16[2,4,4,3584]{3,2,0,1:T(4,128)(2,1)}, u32[]{:S(2)}, u32[]{:S(2)}) async-start(bf16[2,4,4,3584]{3,2,0,1:T(4,128)(2,1)} %pad_maximum_fusion), calls=%async_computation.1 | async-start | bytes 458752 | tf_op jit(solution)/shard_map/all_to_all | solution.py:146
  85.3 2.2 %copy-start.7 = (bf16[1,4,4,3584]{3,2,0,1:T(4,128)(2,1)S(1)}, bf16[1,4,4,3584]{3,2,0,1:T(4,128)(2,1)}, u32[]{:S(2)}) copy-start(bf16[1,4,4,3584]{3,2,0,1:T(4,128)(2,1)} %get-tuple-element.9) | copy-start | bytes 344068
  87.5 7.7 %collective-permute-start.2 = (f32[128,1792]{1,0:T(8,128)}, f32[128,1792]{1,0:T(8,128)S(1)}, u32[]{:S(2)}, u32[]{:S(2)}) collective-permute-start(f32[128,1792]{1,0:T(8,128)} %constant_dynamic-slice_fusion), channel_id=1, source_target_pairs={{1,0},{0,1},{3,2},{2,3},{5,4},{4,5},{7,6},{6,7},{9,8},{8,9},{11,10... | collective-permute-start | bytes 2752520 | tf_op jit(solution)/shard_map/ppermute | solution.py:10
  87.6 1.5 %copy-start.6 = (f32[128,3584]{1,0:T(8,128)S(1)}, f32[128,3584]{1,0:T(8,128)}, u32[]{:S(2)}) copy-start(f32[128,3584]{1,0:T(8,128)} %fusion.11) | copy-start | bytes 5505028
  92.4 1.3 %copy-start.4 = (f32[128,3584]{1,0:T(8,128)}, f32[128,3584]{1,0:T(8,128)S(1)}, u32[]{:S(2)}) copy-start(f32[128,3584]{1,0:T(8,128)S(1)} %fusion) | copy-start | bytes 5505028
  94.7 2.9 %collective-permute-start.3 = (f32[128,1792]{1,0:T(8,128)}, f32[128,1792]{1,0:T(8,128)}, u32[]{:S(2)}, u32[]{:S(2)}) collective-permute-start(f32[128,1792]{1,0:T(8,128)} %constant_dynamic-slice_fusion.1), channel_id=1, source_target_pairs={{1,0},{0,1},{3,2},{2,3},{5,4},{4,5},{7,6},{6,7},{9,8},{8,9},{11,10... | collective-permute-start | bytes 2752520 | tf_op jit(solution)/shard_map/ppermute | solution.py:10
  95.2 2.4 %copy-start.5 = (f32[128,3584]{1,0:T(8,128)S(1)}, f32[128,3584]{1,0:T(8,128)}, u32[]{:S(2)}) copy-start(f32[128,3584]{1,0:T(8,128)} %copy-done.4) | copy-start | bytes 5505028
where the time goes:
time: 101 us; the launch traced here: 99.7 us
  matrix products  42.3 us (42%)
  local copies, waits for them, and re-layouts  15.7 us (16%)
  starting transfers between devices  13.9 us (14%)
  waiting for transfers between devices  12.2 us (12%)
  blocking collectives  7.79 us (8%)
  other arithmetic  7.08 us (7%)
    dot_general x6, matrix products, contract_last(): lax.dot_general(left, right, (((1,), (1,)), ((), ())), preferred_element_...  20.8 us
    ppermute x4, waiting for transfers between devices, passed_along(): return lax.ppermute(block, axis, route)  9.2 us
    dot_general x1, matrix products, shared_pass(): shared_out = jnp.dot(hidden, down_w, preferred_element_type=jnp.float32)  6.2 us
    ppermute x4, starting transfers between devices, passed_along(): return lax.ppermute(block, axis, route)  5.64 us
    all_to_all x1, starting transfers between devices, local(): lax.all_to_all(jnp.stack((result, grad_rows)).reshape(2, n_expert, capaci...  4.14 us
    all_to_all x1, starting transfers between devices, local(): lax.all_to_all(parcel, 'expert', split_axis=1, concat_axis=1, tiled=True)  4.1 us
    dot_general x1, matrix products, expert_local(): jnp.dot(hidden, down_w, preferred_element_type=jnp.float32)  3.3 us
    dynamic_slice x2, local copies, waits for them, and re-layouts, other_sums(): piece = lax.dynamic_slice_in_dim(total, to * width, width, axis=1)  3.22 us
  transfers between devices with their start and end apart: 6, of which 4 were waited for; matrix products, arithmetic and copies ran while one was open for 26% of the time, Pallas kernels for 0%

commit v1 on v0

--- a/solution.py
+++ b/solution.py
@@ -143,12 +143,21 @@
     pieces = lax.all_to_all(parcel, "expert", split_axis=1, concat_axis=1, tiled=True)
     rows = pieces.reshape(3, n_expert * capacity, feature_count)
     result, grad_rows = expert_local(rows[0], rows[1], rows[2], gate_w, up_w, down_w)
-    returned = lax.all_to_all(
-        jnp.stack((result, grad_rows)).reshape(2, n_expert, capacity, feature_count),
-        "expert",
-        split_axis=1,
-        concat_axis=1,
-        tiled=True,
+
+    def view_the_sector(block_here, on_dim, axis_k):
+        tile_out = jnp.concatenate(
+            lax.all_to_all(
+                jnp.stack(jnp.split(block_here, lax.axis_size("expert"), on_dim), axis=0),
+                "expert",
+                0,
+                0,
+            ),
+            axis_k,
+        )
+        return tile_out
+
+    returned = view_the_sector(
+        jnp.stack((result, grad_rows)).reshape(2, n_expert, capacity, feature_count), 1, 1
     )
     back = returned.reshape(2, n_expert * capacity, feature_count)
 

time: 101 us -> 106 us (1.050)
  local copies, waits for them, and re-layouts: 15.7 us -> 19.4 us
  matrix products: 42.3 us -> 43.5 us
    another operation x2 -> x3, local copies, waits for them, and re-layouts: 0.97 us -> 3.46 us  [local(): jnp.stack((result, grad_rows)).reshape(2, n_expert, capacity, feature_count)]
    unnamed x16 -> x17, local copies, waits for them, and re-layouts: 2.35 us -> 3.95 us
    dot_general x1, matrix products: 0.38 us -> 1.85 us  [expert_local(): gate_back = jnp.dot(rows_saved, gate_w, preferred_element_type=jnp.float32)]
  transfers between devices with their start and end apart: 6 -> 6, of which waited for: 4 -> 4; matrix products, arithmetic and copies ran while one was open for 26% -> 23% of each run, Pallas kernels for 0% -> 0%
where the time goes in v1:
time: 106 us; the launch traced here: 105 us
  matrix products  43.5 us (41%)
  local copies, waits for them, and re-layouts  19.4 us (18%)
  starting transfers between devices  13.9 us (13%)
  waiting for transfers between devices  12.7 us (12%)
  blocking collectives  7.79 us (7%)
  other arithmetic  7.13 us (7%)
    dot_general x6, matrix products, contract_last(): lax.dot_general(left, right, (((1,), (1,)), ((), ())), preferred_element_...  21.3 us
    ppermute x4, waiting for transfers between devices, passed_along(): return lax.ppermute(block, axis, route)  9.78 us
    dot_general x1, matrix products, shared_pass(): shared_out = jnp.dot(hidden, down_w, preferred_element_type=jnp.float32)  6.19 us
    ppermute x4, starting transfers between devices, passed_along(): return lax.ppermute(block, axis, route)  5.65 us
    all_to_all x1, starting transfers between devices, view_the_sector(): lax.all_to_all(jnp.stack(jnp.split(block_here, lax.axis_size('expert'), o...  4.14 us
    all_to_all x1, starting transfers between devices, local(): lax.all_to_all(parcel, 'expert', split_axis=1, concat_axis=1, tiled=True)  4.09 us
    unnamed x17, local copies, waits for them, and re-layouts  3.95 us
    another operation x3, local copies, waits for them, and re-layouts, local(): jnp.stack((result, grad_rows)).reshape(2, n_expert, capacity, feature_count)  3.46 us
  transfers between devices with their start and end apart: 6, of which 4 were waited for; matrix products, arithmetic and copies ran while one was open for 23% of the time, Pallas kernels for 0%

profile of v1, /device:TPU:0, one launch (start us, length us, event | category | flops | bytes accessed | tf_op | source)
XLA Modules:
  0.0 105.2 jit_solution(9961535169411248471)
XLA Ops:
  0.6 5.1 %collective-permute-start.1 = (bf16[128,1792]{1,0:T(8,128)(2,1)}, bf16[128,1792]{1,0:T(8,128)(2,1)}, u32[]{:S(2)}, u32[]{:S(2)}) collective-permute-start(bf16[128,1792]{1,0:T(8,128)(2,1)} %bitcast.138), channel_id=1, source_target_pairs={{8,0},{16,8},{24,16},{0,24},{9,1},{17,9},{25,17},{1,25},{10,2},{18... | collective-permute-start | bytes 1376264 | tf_op jit(solution)/shard_map/ppermute | solution.py:10
  5.8 0.8 slice_bitcast_fusion.5
  6.6 0.2 select_reduce_fusion
  6.8 2.7 %all-gather = bf16[1,128,3584]{2,1,0:T(8,128)(2,1)S(1)} all-gather(bf16[1,128,1792]{2,1,0:T(8,128)(2,1)} %param.15), channel_id=2, replica_groups=mesh['pipe'=4,'expert'=4,'tensor'=2] {'tensor'}, dimensions={2}, use_global_device_ids=true | all-gather | bytes 1376256 | tf_op jit(solution)/shard_map/all_gather | solution.py:129
  9.8 2.7 %fusion.13 = f32[128,512]{1,0:T(8,128)S(1)} fusion(bf16[1,3584,512]{2,1,0:T(8,128)(2,1)} %param.23, bf16[1,128,3584]{2,1,0:T(8,128)(2,1)S(1)} %all-gather), kind=kOutput, calls=%fused_computation.20 | convolution fusion | flops 469762048 | bytes 4849664 | tf_op jit(solution)/shard_map/dot_general | solution.py:89
  12.5 4.5 %collective-permute-done.1 = bf16[128,1792]{1,0:T(8,128)(2,1)} collective-permute-done((bf16[128,1792]{1,0:T(8,128)(2,1)}, bf16[128,1792]{1,0:T(8,128)(2,1)}, u32[]{:S(2)}, u32[]{:S(2)}) %collective-permute-start.1) | collective-permute-done | bytes 458784 | tf_op jit(solution)/shard_map/ppermute | solution.py:10
  17.0 2.7 %all_gather.11 = bf16[128,3584]{1,0:T(8,128)(2,1)S(1)} all-gather(bf16[128,1792]{1,0:T(8,128)(2,1)} %collective-permute-done.1), channel_id=1, replica_groups=mesh['pipe'=4,'expert'=4,'tensor'=2] {'tensor'}, dimensions={1}, use_global_device_ids=true | all-gather | bytes 1376256 | tf_op jit(solution)/shard_map/all_gather | solution.py:131
  19.7 0.9 copy-done.2
  20.6 0.2 fusion.2
  20.8 0.7 stack.38
  21.5 5.0 %collective-permute-done = bf16[128,1792]{1,0:T(8,128)(2,1)S(1)} collective-permute-done((bf16[128,1792]{1,0:T(8,128)(2,1)}, bf16[128,1792]{1,0:T(8,128)(2,1)S(1)}, u32[]{:S(2)}, u32[]{:S(2)}) %collective-permute-start) | collective-permute-done | bytes 458784 | tf_op jit(solution)/shard_map/ppermute | solution.py:10
  26.5 2.5 %all_gather.9 = bf16[128,3584]{1,0:T(8,128)(2,1)S(1)} all-gather(bf16[128,1792]{1,0:T(8,128)(2,1)S(1)} %collective-permute-done), channel_id=1, replica_groups=mesh['pipe'=4,'expert'=4,'tensor'=2] {'tensor'}, dimensions={1}, use_global_device_ids=true | all-gather | bytes 1376256 | tf_op jit(solution)/shard_map/all_gather | solution.py:130
  29.2 1.0 maximum_bitcast_fusion
  30.2 0.8 broadcast_in_dim.69
  31.1 4.1 %all-to-all-start = ((bf16[3,4,4,3584]{3,2,0,1:T(4,128)(2,1)}), bf16[3,4,4,3584]{3,2,0,1:T(4,128)(2,1)}, u32[]{:S(2)}, u32[]{:S(2)}) async-start(bf16[3,4,4,3584]{3,2,0,1:T(4,128)(2,1)} %bitcast.11), calls=%async_computation | async-start | bytes 688128 | tf_op jit(solution)/shard_map/all_to_all | solution.py:143
  35.2 3.6 %fusion.3 = f32[128,512]{1,0:T(8,128)S(1)} fusion(bf16[128,3584]{1,0:T(8,128)(2,1)} %copy-done.2, bf16[1,512,3584]{2,1,0:T(8,128)(2,1)} %param.25), kind=kOutput, calls=%fused_computation.10 | convolution fusion | flops 469762048 | bytes 4849664 | tf_op jit(solution)/shard_map/dot_general | solution.py:23
  38.8 6.6 %fusion.11 = f32[128,3584]{1,0:T(8,128)} fusion(bf16[1,3584,512]{2,1,0:T(8,128)(2,1)} %param.23, f32[128,512]{1,0:T(8,128)S(1)} %fusion.3, bf16[1,3584,512]{2,1,0:T(8,128)(2,1)} %param.24, bf16[1,128,3584]{2,1,0:T(8,128)(2,1)} %copy-done.1, f32[128,512]{1,0:T(8,128)S(1)} %fusion.13), kind=kOutput, calls=%fused_computation.18 | convolution fusion | flops 940179456 | bytes 10616832 | tf_op jit(solution)/shard_map/dot_general | solution.py:23
  45.3 1.8 %fusion.112 = (bf16[1,4,4,3584]{3,2,0,1:T(4,128)(2,1)S(1)}, bf16[1,4,4,3584]{3,2,0,1:T(4,128)(2,1)}, bf16[1,4,4,3584]{3,2,0,1:T(4,128)(2,1)}) fusion(bf16[3,4,4,3584]{3,2,0,1:T(4,128)(2,1)} %all-to-all-done), kind=kLoop, calls=%fused_computation.129 | loop fusion | bytes 688128 | tf_op jit(solution)/shard_map/slice | solution.py:145
  47.1 0.9 squeeze.52
  48.1 1.8 %fusion.29 = f32[16,256]{1,0:T(8,128)S(1)} fusion(bf16[16,3584]{1,0:T(8,128)(2,1)S(1)} %squeeze.52, bf16[1,1,3584,256]{3,2,1,0:T(8,128)(2,1)} %param.20), kind=kOutput, calls=%fused_computation.36 | convolution fusion | flops 29360128 | bytes 1966080 | tf_op jit(solution)/shard_map/dot_general | solution.py:69
  49.9 3.3 %convolution_convert_fusion = bf16[16,3584]{1,0:T(8,128)(2,1)} fusion(bf16[1,1,256,3584]{3,2,1,0:T(8,128)(2,1)} %param.22, bf16[16,3584]{1,0:T(8,128)(2,1)S(1)} %squeeze.52, bf16[1,1,3584,256]{3,2,1,0:T(8,128)(2,1)S(1)} %copy-done, f32[16,256]{1,0:T(8,128)S(1)} %fusion.29), kind=kOutput, calls=%fused_computation.5 | convolution fusion | flops 58802176 | bytes 3915776 | tf_op jit(solution)/shard_map/dot_general | solution.py:72
  53.2 0.9 stack.40
  54.2 0.7 constant_dynamic-update-slice_fusion.1
  54.8 0.9 squeeze.56
  55.8 2.1 %fusion.17 = f32[16,256]{1,0:T(8,128)S(1)} fusion(bf16[16,3584]{1,0:T(8,128)(2,1)S(1)} %squeeze.56, bf16[1,1,256,3584]{3,2,1,0:T(8,128)(2,1)} %param.22), kind=kOutput, calls=%fused_computation.24 | convolution fusion | flops 29360128 | bytes 1966080 | tf_op jit(solution)/shard_map/dot_general | solution.py:23
  57.9 1.8 %fusion.27 = f32[16,256]{1,0:T(8,128)S(1)} fusion(bf16[16,3584]{1,0:T(8,128)(2,1)S(1)} %squeeze.57, bf16[1,1,3584,256]{3,2,1,0:T(8,128)(2,1)} %param.20), kind=kOutput, calls=%fused_computation.34 | convolution fusion | flops 29360128 | bytes 1966080 | tf_op jit(solution)/shard_map/dot_general | solution.py:73
  59.8 3.5 %fusion.25 = f32[16,3584]{1,0:T(8,128)} fusion(bf16[1,1,3584,256]{3,2,1,0:T(8,128)(2,1)} %param.20, f32[16,256]{1,0:T(8,128)S(1)} %fusion.17, bf16[16,3584]{1,0:T(8,128)(2,1)S(1)} %squeeze.57, bf16[1,1,3584,256]{3,2,1,0:T(8,128)(2,1)S(1)} %copy-done, f32[16,256]{1,0:T(8,128)S(1)} %fusion.27), kind=kOutput, calls=%fused_computation.32 | convolution fusion | flops 58761216 | bytes 4046848 | tf_op jit(solution)/shard_map/dot_general | solution.py:23
  63.2 2.2 %fusion.1 = bf16[16,3584]{1,0:T(8,128)(2,1)} fusion(f32[16,3584]{1,0:T(8,128)} %fusion.25, bf16[1,1,3584,256]{3,2,1,0:T(8,128)(2,1)S(1)} %copy-done, f32[16,256]{1,0:T(8,128)S(1)} %fusion.17, f32[16,256]{1,0:T(8,128)S(1)} %fusion.27), kind=kOutput, calls=%fused_computation.4 | convolution fusion | flops 29499392 | bytes 2211840 | tf_op jit(solution)/shard_map/dot_general | solution.py:23
  65.4 1.6 %stack.41 = bf16[1,4,4,3584]{3,2,1,0:T(4,128)(2,1)} reshape(bf16[16,3584]{1,0:T(8,128)(2,1)} %fusion.1) | data formatting | bytes 229376 | tf_op jit(solution)/shard_map/stack | solution.py:160
  67.0 1.0 constant_dynamic-update-slice_fusion
  68.1 0.9 pad_maximum_fusion
  69.0 4.1 %all-to-all-start.1 = ((bf16[4,2,1,4,3584]{4,3,1,2,0:T(4,128)(2,1)}), bf16[4,2,1,4,3584]{4,3,1,2,0:T(4,128)(2,1)}, u32[]{:S(2)}, u32[]{:S(2)}) async-start(bf16[4,2,1,4,3584]{4,3,1,2,0:T(4,128)(2,1)} %pad_maximum_fusion), calls=%async_computation.1 | async-start | bytes 458752 | tf_op jit(solution)/shard_map/all_to_all | solution.py:149
  73.1 2.7 %fusion.9 = f32[128,512]{1,0:T(8,128)S(1)} fusion(bf16[128,3584]{1,0:T(8,128)(2,1)S(1)} %all_gather.9, bf16[1,3584,512]{2,1,0:T(8,128)(2,1)} %param.24), kind=kOutput, calls=%fused_computation.16 | convolution fusion | flops 469762048 | bytes 4849664 | tf_op jit(solution)/shard_map/dot_general | solution.py:86
  75.8 2.9 %all-to-all-done.1 = bf16[4,2,1,4,3584]{4,3,1,2,0:T(4,128)(2,1)} async-done(((bf16[4,2,1,4,3584]{4,3,1,2,0:T(4,128)(2,1)}), bf16[4,2,1,4,3584]{4,3,1,2,0:T(4,128)(2,1)}, u32[]{:S(2)}, u32[]{:S(2)}) %all-to-all-start.1) | async-done | bytes 229408 | tf_op jit(solution)/shard_map/all_to_all | solution.py:149
  78.7 1.7 %fusion.113 = (bf16[1,4,1,4,3584]{4,3,0,2,1:T(4,128)(2,1)}, bf16[1,4,1,4,3584]{4,3,0,2,1:T(4,128)(2,1)}) fusion(bf16[2,4,1,4,3584]{4,3,0,2,1:T(4,128)(2,1)} %bitcast.19), kind=kLoop, calls=%fused_computation.130 | loop fusion | bytes 458752 | tf_op jit(solution)/shard_map/slice | solution.py:172
  80.4 1.6 %squeeze.58 = bf16[16,3584]{1,0:T(8,128)(2,1)} reshape(bf16[1,4,1,4,3584]{4,3,0,2,1:T(4,128)(2,1)} %get-tuple-element.10) | data formatting | bytes 229376 | tf_op jit(solution)/shard_map/squeeze | solution.py:171
  82.0 2.6 %fusion.71 = f32[128,3584]{1,0:T(8,128)} fusion(bf16[16,3584]{1,0:T(8,128)(2,1)} %squeeze.58, bf16[16,128]{1,0:T(8,128)(2,1)S(1)} %bitcast.134, bf16[16,128]{1,0:T(8,128)(2,1)S(1)} %bitcast.135), kind=kOutput, calls=%fused_computation.61 | convolution fusion | flops 29835264 | bytes 1957888 | tf_op jit(solution)/shard_map/dot_general | solution.py:52
  84.7 6.2 %convolution_add_fusion.1 = f32[128,3584]{1,0:T(8,128)} fusion(f32[128,3584]{1,0:T(8,128)} %fusion.71, bf16[1,512,3584]{2,1,0:T(8,128)(2,1)} %param.25, f32[128,512]{1,0:T(8,128)S(1)} %fusion.9, bf16[128,3584]{1,0:T(8,128)(2,1)S(1)} %all_gather.9, bf16[1,3584,512]{2,1,0:T(8,128)(2,1)} %param.23), kind=kOutput, calls=%fused_computation.2 | convolution fusion | flops 940376064 | bytes 12189696 | tf_op jit(solution)/shard_map/dot_general | solution.py:88
  90.9 2.2 %constant_dynamic-slice_fusion = f32[128,1792]{1,0:T(8,128)} fusion(f32[128,3584]{1,0:T(8,128)} %convolution_add_fusion.1, s32[]{:T(128)S(6)} %select_n.74), kind=kLoop, calls=%fused_computation.119 | loop fusion | bytes 1835012 | tf_op jit(solution)/shard_map/dynamic_slice | solution.py:63
  93.1 0.4 fusion.114
  93.6 1.1 %copy-done.5 = f32[128,3584]{1,0:T(8,128)S(1)} copy-done((f32[128,3584]{1,0:T(8,128)S(1)}, f32[128,3584]{1,0:T(8,128)}, u32[]{:S(2)}) %copy-start.5) | copy-done | bytes 1835032
  94.6 3.3 %fusion = f32[128,3584]{1,0:T(8,128)S(1)} fusion(f32[128,3584]{1,0:T(8,128)S(1)} %fusion.114, f32[128,3584]{1,0:T(8,128)S(1)} %copy-done.5, bf16[1,3584,512]{2,1,0:T(8,128)(2,1)} %param.24, f32[128,512]{1,0:T(8,128)S(1)} %fusion.3, f32[128,512]{1,0:T(8,128)S(1)} %fusion.13), kind=kOutput, calls=%fused_computation.1 | convolution fusion | flops 471072768 | bytes 9699328 | tf_op jit(solution)/shard_map/dot_general | solution.py:23
  98.0 1.2 %copy-done.3 = f32[128,3584]{1,0:T(8,128)} copy-done((f32[128,3584]{1,0:T(8,128)}, f32[128,3584]{1,0:T(8,128)S(1)}, u32[]{:S(2)}) %copy-start.3) | copy-done | bytes 1835032
  99.2 1.0 constant_dynamic-slice_fusion.1
  100.2 0.5 collective-permute-start.3
  100.8 2.2 %fusion.65 = bf16[1,128,1792]{2,1,0:T(8,128)(2,1)} fusion(f32[128,1792]{1,0:T(8,128)S(1)} %collective-permute-done.2, f32[128,3584]{1,0:T(8,128)} %convolution_add_fusion.1, s32[]{:T(128)S(6)} %select_n.72), kind=kLoop, calls=%fused_computation.51 | loop fusion | flops 458752 | bytes 2293764 | tf_op jit(solution)/shard_map/broadcast_in_dim | solution.py:178
  102.9 0.3 collective-permute-done.3
  103.2 2.0 %fusion.66 = bf16[1,128,1792]{2,1,0:T(8,128)(2,1)} fusion(f32[128,1792]{1,0:T(8,128)} %collective-permute-done.3, f32[128,3584]{1,0:T(8,128)S(1)} %copy-done.4, s32[]{:T(128)S(6)} %select_n.72), kind=kLoop, calls=%fused_computation.52 | loop fusion | flops 458752 | bytes 2293764 | tf_op jit(solution)/shard_map/broadcast_in_dim | solution.py:178
  (32 shorter events, 0.8 us)
Async XLA Ops:
  0.6 49.3 %copy-start = (bf16[1,1,3584,256]{3,2,1,0:T(8,128)(2,1)S(1)}, bf16[1,1,3584,256]{3,2,1,0:T(8,128)(2,1)}, u32[]{:S(2)}) copy-start(bf16[1,1,3584,256]{3,2,1,0:T(8,128)(2,1)} %param.21) | copy-start | bytes 5505028
  0.6 16.4 %collective-permute-start.1 = (bf16[128,1792]{1,0:T(8,128)(2,1)}, bf16[128,1792]{1,0:T(8,128)(2,1)}, u32[]{:S(2)}, u32[]{:S(2)}) collective-permute-start(bf16[128,1792]{1,0:T(8,128)(2,1)} %bitcast.138), channel_id=1, source_target_pairs={{8,0},{16,8},{24,16},{0,24},{9,1},{17,9},{25,17},{1,25},{10,2},{18... | collective-permute-start | bytes 1376264 | tf_op jit(solution)/shard_map/ppermute | solution.py:10
  5.8 20.7 %collective-permute-start = (bf16[128,1792]{1,0:T(8,128)(2,1)}, bf16[128,1792]{1,0:T(8,128)(2,1)S(1)}, u32[]{:S(2)}, u32[]{:S(2)}) collective-permute-start(bf16[128,1792]{1,0:T(8,128)(2,1)} %bitcast.139), channel_id=1, source_target_pairs={{24,0},{0,8},{8,16},{16,24},{25,1},{1,9},{9,17},{17,25},{26,2},{2,... | collective-permute-start | bytes 1376264 | tf_op jit(solution)/shard_map/ppermute | solution.py:10
  9.5 3.0 %copy-start.1 = (bf16[1,128,3584]{2,1,0:T(8,128)(2,1)}, bf16[1,128,3584]{2,1,0:T(8,128)(2,1)S(1)}, u32[]{:S(2)}) copy-start(bf16[1,128,3584]{2,1,0:T(8,128)(2,1)S(1)} %all-gather) | copy-start | bytes 2752516
  19.7 0.9 copy-start.2
  31.1 14.3 %all-to-all-start = ((bf16[3,4,4,3584]{3,2,0,1:T(4,128)(2,1)}), bf16[3,4,4,3584]{3,2,0,1:T(4,128)(2,1)}, u32[]{:S(2)}, u32[]{:S(2)}) async-start(bf16[3,4,4,3584]{3,2,0,1:T(4,128)(2,1)} %bitcast.11), calls=%async_computation | async-start | bytes 688128 | tf_op jit(solution)/shard_map/all_to_all | solution.py:143
  63.2 3.8 %copy-start.6 = (bf16[2,4,4,3584]{3,2,1,0:T(4,128)(2,1)S(1)}, bf16[2,4,4,3584]{3,2,1,0:T(4,128)(2,1)}, u32[]{:S(2)}) copy-start(bf16[2,4,4,3584]{3,2,1,0:T(4,128)(2,1)} %constant_dynamic-update-slice_fusion.1) | copy-start | bytes 688132
  69.0 9.8 %all-to-all-start.1 = ((bf16[4,2,1,4,3584]{4,3,1,2,0:T(4,128)(2,1)}), bf16[4,2,1,4,3584]{4,3,1,2,0:T(4,128)(2,1)}, u32[]{:S(2)}, u32[]{:S(2)}) async-start(bf16[4,2,1,4,3584]{4,3,1,2,0:T(4,128)(2,1)} %pad_maximum_fusion), calls=%async_computation.1 | async-start | bytes 458752 | tf_op jit(solution)/shard_map/all_to_all | solution.py:149
  90.9 2.2 %copy-start.7 = (bf16[1,4,1,4,3584]{4,3,0,2,1:T(4,128)(2,1)S(1)}, bf16[1,4,1,4,3584]{4,3,0,2,1:T(4,128)(2,1)}, u32[]{:S(2)}) copy-start(bf16[1,4,1,4,3584]{4,3,0,2,1:T(4,128)(2,1)} %get-tuple-element.9) | copy-start | bytes 344068
  93.1 7.7 %collective-permute-start.2 = (f32[128,1792]{1,0:T(8,128)}, f32[128,1792]{1,0:T(8,128)S(1)}, u32[]{:S(2)}, u32[]{:S(2)}) collective-permute-start(f32[128,1792]{1,0:T(8,128)} %constant_dynamic-slice_fusion), channel_id=1, source_target_pairs={{1,0},{0,1},{3,2},{2,3},{5,4},{4,5},{7,6},{6,7},{9,8},{8,9},{11,10... | collective-permute-start | bytes 2752520 | tf_op jit(solution)/shard_map/ppermute | solution.py:10
  93.1 1.5 %copy-start.5 = (f32[128,3584]{1,0:T(8,128)S(1)}, f32[128,3584]{1,0:T(8,128)}, u32[]{:S(2)}) copy-start(f32[128,3584]{1,0:T(8,128)} %fusion.11) | copy-start | bytes 5505028
  98.0 1.3 %copy-start.3 = (f32[128,3584]{1,0:T(8,128)}, f32[128,3584]{1,0:T(8,128)S(1)}, u32[]{:S(2)}) copy-start(f32[128,3584]{1,0:T(8,128)S(1)} %fusion) | copy-start | bytes 5505028
  100.2 3.0 %collective-permute-start.3 = (f32[128,1792]{1,0:T(8,128)}, f32[128,1792]{1,0:T(8,128)}, u32[]{:S(2)}, u32[]{:S(2)}) collective-permute-start(f32[128,1792]{1,0:T(8,128)} %constant_dynamic-slice_fusion.1), channel_id=1, source_target_pairs={{1,0},{0,1},{3,2},{2,3},{5,4},{4,5},{7,6},{6,7},{9,8},{8,9},{11,10... | collective-permute-start | bytes 2752520 | tf_op jit(solution)/shard_map/ppermute | solution.py:10
  100.7 2.4 %copy-start.4 = (f32[128,3584]{1,0:T(8,128)S(1)}, f32[128,3584]{1,0:T(8,128)}, u32[]{:S(2)}) copy-start(f32[128,3584]{1,0:T(8,128)} %copy-done.3) | copy-start | bytes 5505028
